TPU v7x, 256 devices: a whole 4x4x8 slice. The times are simulated.
256 devices in a mesh: rows: 64 (over x, z_hi, y, core), feat: 4 (over z_lo).
Axes of the slice: x: 4, y: 4, z: 8 (z_hi: 2, z_lo: 4; z = z_hi * 4 + z_lo), core: 2. Of those that a mesh axis runs over, the one named last changes fastest.
Arguments:
- bins: int32 [65536, 512], P('rows', 'feat'), may hold values from -2147483648 to 2147483647, as said below
- hessian: float32 [262144], P('rows'), may hold values from 0.05 to 1
- thresholds: float32 [128], replicated, may hold values from 0.02 to 0.98
Outputs:
- cuts: float32 [512, 128], P('feat')
Inputs may be any that keep to these rules, and one draw needn't show every extreme that they name: `bins`: each word holds the bin ids, 0 to 255, of rows 4i to 4i + 3 of one feature, row 4i + k in bits 8k to 8k + 7 of the two's complement word.
All inputs are finite; a program needn't handle non-finite values.
Results may differ from a plain program's by a relative error of at most 0.000065.
Values sent between devices are 32-bit elements; how exact they have to be, the bound alone decides.
A program may use at most 192 MiB of HBM per device.

v0:
```python
import functools

import jax
import jax.numpy as jnp
from jax import lax
from jax.experimental import pallas as pl
from jax.experimental.pallas import tpu as pltpu
from jax.sharding import PartitionSpec as P

BINS = 256
LEVELS = 16
GROUP = 16
LANES = 128
CHUNK = 256
MESH = pl.DeviceIdType.MESH


def kernel(ranks, bins_hbm, hess_hbm, thr_hbm, out_ref, bins_ref, hess_ref, thr_ref, prefix, column_ref, cols, wts, stage, inbox, mine, load_sem, send_sem, recv_sem, gather_send, gather_recv):
    words, width = bins_ref.shape
    tiles = words // LANES
    hess_load = pltpu.make_async_copy(hess_hbm, hess_ref, load_sem.at[tiles])
    hess_load.start()
    bins_loads = []
    for t in range(tiles):
        part = pl.ds(t * LANES, LANES)
        bins_loads.append(pltpu.make_async_copy(bins_hbm.at[part, :], bins_ref.at[part, :], load_sem.at[t]))
        bins_loads[t].start()
    thr_load = pltpu.make_async_copy(thr_hbm, thr_ref, load_sem.at[tiles + 1])
    thr_load.start()
    groups = width // GROUP
    replicas = ranks // groups
    lanes = LEVELS * GROUP
    me = lax.axis_index("rows")
    team, seat = me // groups, me % groups

    barrier = pltpu.get_barrier_semaphore()
    for step in range(1, ranks):
        pl.semaphore_signal(barrier, inc=1, device_id={"rows": (me + step) % ranks}, device_id_type=MESH)

    src = lax.broadcasted_iota(jnp.int32, (lanes, lanes), 0)
    dst = lax.broadcasted_iota(jnp.int32, (lanes, lanes), 1)
    gap = dst - src
    same = jnp.bitwise_and(gap, GROUP - 1) == 0
    prefix[:, :lanes] = jnp.where(jnp.logical_and(same, gap > 0), 1.0, 0.0).astype(jnp.bfloat16)
    prefix[:, lanes:] = jnp.where(same, 1.0, 0.0).astype(jnp.bfloat16)

    row = lax.broadcasted_iota(jnp.int32, (LANES, LANES), 0)
    col = lax.broadcasted_iota(jnp.int32, (LANES, LANES), 1)
    quarter = LANES // 4
    order = jnp.where(row == 4 * (col % quarter) + col // quarter, 1.0, 0.0).astype(jnp.bfloat16)
    lane = lax.broadcasted_iota(jnp.int32, (2 * tiles, LANES), 1) // quarter
    hess_load.wait()
    flat = jnp.concatenate([hess_ref[pl.ds(j, tiles, stride=4), :] for j in range(4)], axis=0)
    left_factor = jnp.ones_like(flat)
    miss = jnp.abs(flat - flat.astype(jnp.bfloat16).astype(jnp.float32))
    for j in range(1, 128, 2):
        factor = 1.0 + j / 128.0
        other = (flat * (1.0 / factor)).astype(jnp.bfloat16).astype(jnp.float32)
        away = jnp.abs(flat - other * factor)
        left_factor = jnp.where(away < miss, factor, left_factor)
        miss = jnp.minimum(miss, away)
    right_factor = flat / left_factor
    for t in range(tiles):
        bins_loads[t].wait()
    thr_load.wait()
    for t in range(tiles):
        cols[:, t * LANES : (t + 1) * LANES] = bins_ref[t * LANES : (t + 1) * LANES, :].T
    column_ref[...] = jnp.broadcast_to(thr_ref[...], (LANES, thr_ref.shape[1])).T
    pieces = jnp.concatenate([x[j * tiles : (j + 1) * tiles] for j in range(4) for x in (left_factor, right_factor)], axis=0)
    moved = jnp.dot(pieces.astype(jnp.bfloat16), order, preferred_element_type=jnp.float32)
    for k in range(4):
        plane = None
        for j in range(4):
            block = moved[2 * tiles * j : 2 * tiles * (j + 1)]
            if j != k:
                block = pltpu.roll(block, (quarter * (j - k)) % LANES, 1)
            plane = block if plane is None else jnp.where(lane == j, block, plane)
        for piece in range(2):
            for t in range(tiles):
                line = plane[piece * tiles + t : piece * tiles + t + 1]
                wts[piece, k, :, t * LANES : (t + 1) * LANES] = jnp.broadcast_to(line, (GROUP, LANES)).astype(jnp.bfloat16)

    def peer(step):
        place, bit = 0, 1
        while bit < groups:
            place = place + (seat // bit + step // bit) % 2 * bit
            bit *= 2
        return place

    def group_hist(group):
        base = pl.multiple_of(group * GROUP, GROUP)
        zero = jnp.zeros((GROUP, CHUNK), jnp.bfloat16)
        sums = [None, None]
        index = 0
        for c in range(words // CHUNK):
            part = cols[pl.ds(base, GROUP), c * CHUNK : (c + 1) * CHUNK]
            for k in range(4):
                high = jnp.bitwise_and(jnp.right_shift(part, 8 * k + 4), 15).astype(jnp.float32).astype(jnp.bfloat16)
                low = jnp.bitwise_and(jnp.right_shift(part, 8 * k), 15).astype(jnp.float32).astype(jnp.bfloat16)
                w0 = wts[0, k, :, c * CHUNK : (c + 1) * CHUNK]
                w1 = wts[1, k, :, c * CHUNK : (c + 1) * CHUNK]
                left = jnp.concatenate([jnp.where(high == jnp.bfloat16(h), w0, zero) for h in range(LEVELS)], axis=0)
                right = jnp.concatenate([jnp.where(low == jnp.bfloat16(l), w1, zero) for l in range(LEVELS)], axis=0)
                part_sum = lax.dot_general(left, right, (((1,), (1,)), ((), ())), preferred_element_type=jnp.float32)
                side = index % 2
                sums[side] = part_sum if sums[side] is None else sums[side] + part_sum
                index += 1
        joint = sums[0] + sums[1]
        own_row = lax.broadcasted_iota(jnp.int32, (GROUP, lanes), 0)
        own_col = lax.broadcasted_iota(jnp.int32, (GROUP, lanes), 1)
        keep = own_row == own_col % GROUP
        lines = []
        for h in range(LEVELS):
            lines.append(jnp.sum(jnp.where(keep, joint[h * GROUP : (h + 1) * GROUP], 0.0), axis=0, keepdims=True))
        return jnp.concatenate(lines, axis=0)

    def outgoing(step, e):
        target = ((team + e) % replicas) * groups + peer(step)
        slot = step * replicas + e
        return pltpu.make_async_remote_copy(
            src_ref=stage.at[step],
            dst_ref=inbox.at[slot],
            send_sem=send_sem.at[slot],
            recv_sem=recv_sem.at[slot],
            device_id={"rows": target},
            device_id_type=MESH,
        )

    def do_pair(turn, carry):
        step = groups - 1 - 2 * turn
        first = group_hist(peer(step))
        second = group_hist(peer(step - 1))
        stage[step] = first
        stage[step - 1] = second

        @pl.when(turn == 0)
        def _():
            pl.semaphore_wait(barrier, ranks - 1)

        for e in range(replicas):
            outgoing(step, e).start()

        @pl.when(turn < groups // 2 - 1)
        def _():
            for e in range(replicas):
                outgoing(step - 1, e).start()

        return carry

    lax.fori_loop(0, groups // 2, do_pair, 0)
    for e in range(1, replicas):
        outgoing(0, e).start()

    total = stage[0]
    for step in reversed(range(groups)):
        for e in range(replicas):
            if step + e > 0:
                outgoing(step, e).wait()
                total = total + inbox[step * replicas + e]

    p0 = total.astype(jnp.bfloat16).astype(jnp.float32)
    p1 = (total - p0).astype(jnp.bfloat16).astype(jnp.float32)
    p2 = total - p0 - p1
    split = jnp.concatenate([p0, p1, p2], axis=0).astype(jnp.bfloat16)
    sums3 = jnp.dot(split, prefix[...], preferred_element_type=jnp.float32)
    inner3, level3 = sums3[:, :lanes], sums3[:, lanes:]
    inner = inner3[:LEVELS] + inner3[LEVELS : 2 * LEVELS] + inner3[2 * LEVELS :]
    level = level3[:LEVELS] + level3[LEVELS : 2 * LEVELS] + level3[2 * LEVELS :]
    inv = 1.0 / (total + 1.0)
    whole = jnp.sum(level, axis=0, keepdims=True)
    target = column_ref[...] * whole[:, :LANES]
    run = jnp.zeros((1, lanes), jnp.float32)
    acc = jnp.zeros((thr_ref.shape[1], LANES), jnp.float32)
    for h in range(LEVELS):
        before = inner[h : h + 1] + run
        run = run + level[h : h + 1]
        for t in range(lanes // LANES):
            cut = slice(t * LANES, (t + 1) * LANES)
            ratio = (target - before[:, cut]) * inv[h : h + 1, cut]
            acc = acc + jnp.clip(ratio, 0.0, 1.0)
    turned = acc.T
    cuts = turned[:GROUP]
    for j in range(1, LANES // GROUP):
        cuts = cuts + turned[j * GROUP : (j + 1) * GROUP]
    mine[...] = cuts
    here = pl.multiple_of(seat * GROUP, GROUP)

    def spread(step):
        return pltpu.make_async_remote_copy(
            src_ref=mine,
            dst_ref=out_ref.at[pl.ds(here, GROUP), :],
            send_sem=gather_send.at[step],
            recv_sem=gather_recv.at[step],
            device_id={"rows": team * groups + peer(step)},
            device_id_type=MESH,
        )

    for step in reversed(range(1, groups)):
        spread(step).start()
    out_ref[pl.ds(here, GROUP), :] = cuts
    for step in range(1, groups):
        spread(step).wait()


def solution(mesh):
    ranks = mesh.shape["rows"]

    def local(bins, hessian, thresholds):
        words, width = bins.shape
        groups = width // GROUP
        quantiles = thresholds.shape[0]
        lanes = LEVELS * GROUP
        return pl.pallas_call(
            functools.partial(kernel, ranks),
            out_shape=pltpu.VMEM((width, quantiles), jnp.float32),
            in_specs=[pl.BlockSpec(memory_space=pl.ANY)] * 3,
            out_specs=pl.BlockSpec(memory_space=pltpu.VMEM),
            scratch_shapes=[
                pltpu.VMEM((words, width), jnp.int32),
                pltpu.VMEM((4 * words // LANES, LANES), jnp.float32),
                pltpu.VMEM((1, quantiles), jnp.float32),
                pltpu.VMEM((lanes, 2 * lanes), jnp.bfloat16),
                pltpu.VMEM((quantiles, LANES), jnp.float32),
                pltpu.VMEM((width, words), jnp.int32),
                pltpu.VMEM((2, 4, GROUP, words), jnp.bfloat16),
                pltpu.VMEM((groups, LEVELS, lanes), jnp.float32),
                pltpu.VMEM((ranks, LEVELS, lanes), jnp.float32),
                pltpu.VMEM((GROUP, quantiles), jnp.float32),
                pltpu.SemaphoreType.DMA((words // LANES + 2,)),
                pltpu.SemaphoreType.DMA((ranks,)),
                pltpu.SemaphoreType.DMA((ranks,)),
                pltpu.SemaphoreType.DMA((groups,)),
                pltpu.SemaphoreType.DMA((groups,)),
            ],
            compiler_params=pltpu.CompilerParams(collective_id=0, has_side_effects=True),
        )(bins, hessian.reshape(-1, LANES), thresholds.reshape(1, -1))

    in_specs = (P("rows", "feat"), P("rows"), P())
    return jax.shard_map(local, mesh=mesh, in_specs=in_specs, out_specs=P("feat", None), check_vma=False)
```

profile of v0, /device:TPU:33, one launch (start us, length us, event | category | flops | bytes accessed | tf_op | source)
XLA Modules:
  0.0 42.0 jit_solution(7649897466243215266)
XLA Ops:
  0.0 41.3 %shard_map.37 = f32[128,128]{1,0:T(8,128)S(1)} custom-call(s32[1024,128]{1,0:T(8,128)} %bins_hbm.1, f32[32,128]{1,0:T(8,128)} %bitcast.2, f32[1,128]{1,0:T(1,128)} %bitcast.3), custom_call_target="tpu_custom_call" | custom-call | tf_op jit(solution)/shard_map/pallas_call | solution.py:213
  41.3 0.6 %copy.5 = f32[128,128]{1,0:T(8,128)} copy(f32[128,128]{1,0:T(8,128)S(1)} %shard_map.37) | data formatting | bytes 131072
where the time goes:
time: 42.1 us; the launch traced here: 42 us
  Pallas kernels  41.3 us (98%)
  local copies, waits for them, and re-layouts  0.63 us (1%)
    pallas_call x1, Pallas kernels, local(): pl.pallas_call(functools.partial(kernel, ranks), out_shape=pltpu.VMEM((wi...  41.3 us

commit v1 on v0

v1 whole, which is shorter than its diff:
```python
import jax
import jax.numpy as jnp
from jax import lax
from jax.experimental import pallas as pl
from jax.experimental.pallas import tpu as pltpu
from jax.sharding import PartitionSpec as P

LEVELS = 16
GROUP = 16
OCTET = 8
LANES = 128
CHUNK = 256
NX, NZ, NY, NC = 4, 2, 4, 2
RANKS = NX * NZ * NY * NC
SEATS = NX * NY
STEPS = SEATS // 2
MESH = pl.DeviceIdType.MESH


def kernel(bins_hbm, hess_hbm, thr_hbm, out_ref, bins_ref, hess_ref, thr_ref, prefix, column_ref, cols, wts, stage, inbox, mine, load_sem, send_sem, recv_sem, gather_send, gather_recv):
    words, width = bins_ref.shape
    tiles = words // LANES
    hess_load = pltpu.make_async_copy(hess_hbm, hess_ref, load_sem.at[tiles])
    hess_load.start()
    bins_loads = []
    for t in range(tiles):
        part = pl.ds(t * LANES, LANES)
        bins_loads.append(pltpu.make_async_copy(bins_hbm.at[part, :], bins_ref.at[part, :], load_sem.at[t]))
        bins_loads[t].start()
    thr_load = pltpu.make_async_copy(thr_hbm, thr_ref, load_sem.at[tiles + 1])
    thr_load.start()
    me = lax.axis_index("rows")
    x, z, y, core = me // (NZ * NY * NC), me // (NY * NC) % NZ, me // NC % NY, me % NC
    owner = core == NC - 1

    def device(px, pz, py, pc):
        return ((px * NZ + pz) * NY + py) * NC + pc

    barrier = pltpu.get_barrier_semaphore()
    for step in range(1, RANKS):
        pl.semaphore_signal(barrier, inc=1, device_id={"rows": (me + step) % RANKS}, device_id_type=MESH)

    src = lax.broadcasted_iota(jnp.int32, (LANES, LANES), 0)
    dst = lax.broadcasted_iota(jnp.int32, (LANES, LANES), 1)
    gap = dst - src
    same = jnp.bitwise_and(gap, OCTET - 1) == 0
    prefix[:, :LANES] = jnp.where(jnp.logical_and(same, gap > 0), 1.0, 0.0).astype(jnp.bfloat16)
    prefix[:, LANES:] = jnp.where(same, 1.0, 0.0).astype(jnp.bfloat16)

    quarter = LANES // 4
    order = jnp.where(src == 4 * (dst % quarter) + dst // quarter, 1.0, 0.0).astype(jnp.bfloat16)
    lane = lax.broadcasted_iota(jnp.int32, (2 * tiles, LANES), 1) // quarter
    hess_load.wait()
    flat = jnp.concatenate([hess_ref[pl.ds(j, tiles, stride=4), :] for j in range(4)], axis=0)
    left_factor = jnp.ones_like(flat)
    miss = jnp.abs(flat - flat.astype(jnp.bfloat16).astype(jnp.float32))
    for j in range(1, 128, 2):
        factor = 1.0 + j / 128.0
        other = (flat * (1.0 / factor)).astype(jnp.bfloat16).astype(jnp.float32)
        away = jnp.abs(flat - other * factor)
        left_factor = jnp.where(away < miss, factor, left_factor)
        miss = jnp.minimum(miss, away)
    right_factor = flat / left_factor
    for t in range(tiles):
        bins_loads[t].wait()
    thr_load.wait()
    for t in range(tiles):
        cols[:, t * LANES : (t + 1) * LANES] = bins_ref[t * LANES : (t + 1) * LANES, :].T
    column_ref[...] = jnp.broadcast_to(thr_ref[...], (LANES, thr_ref.shape[1])).T
    pieces = jnp.concatenate([x[j * tiles : (j + 1) * tiles] for j in range(4) for x in (left_factor, right_factor)], axis=0)
    moved = jnp.dot(pieces.astype(jnp.bfloat16), order, preferred_element_type=jnp.float32)
    for k in range(4):
        plane = None
        for j in range(4):
            block = moved[2 * tiles * j : 2 * tiles * (j + 1)]
            if j != k:
                block = pltpu.roll(block, (quarter * (j - k)) % LANES, 1)
            plane = block if plane is None else jnp.where(lane == j, block, plane)
        for piece in range(2):
            for t in range(tiles):
                line = plane[piece * tiles + t : piece * tiles + t + 1]
                wts[piece, k, :, t * LANES : (t + 1) * LANES] = jnp.broadcast_to(line, (GROUP, LANES)).astype(jnp.bfloat16)

    sub = lax.broadcasted_iota(jnp.int32, (OCTET, LANES), 0)
    diagonal = sub == lax.broadcasted_iota(jnp.int32, (OCTET, LANES), 1) % OCTET

    def gather_rows(tiles8):
        low4, low2, low1 = sub < 4, sub % 4 < 2, sub % 2 < 1
        four = []
        for a in range(4):
            p, q = tiles8[a], tiles8[a + 4]
            four.append(jnp.where(low4, p, q) + pltpu.roll(jnp.where(low4, q, p), 4, 0))
        two = []
        for a in range(2):
            p, q = four[a], four[a + 2]
            two.append(jnp.where(low2, p, q) + jnp.where(low2, pltpu.roll(p, 6, 0), pltpu.roll(q, 2, 0)))
        p, q = two
        return jnp.where(low1, p, q) + jnp.where(low1, pltpu.roll(p, 7, 0), pltpu.roll(q, 1, 0))

    def group_hist(group):
        base = pl.multiple_of(group * GROUP, GROUP)
        zero = jnp.zeros((GROUP, CHUNK), jnp.bfloat16)
        upper = (lax.broadcasted_iota(jnp.int32, (GROUP, CHUNK), 0) // OCTET)
        sums = [None, None]
        index = 0
        for c in range(words // CHUNK):
            part = cols[pl.ds(base, GROUP), c * CHUNK : (c + 1) * CHUNK]
            for k in range(4):
                high = jnp.bitwise_and(jnp.right_shift(part, 8 * k + 4), 15).astype(jnp.float32).astype(jnp.bfloat16)
                low = jnp.bitwise_and(jnp.right_shift(part, 8 * k), 15)
                w0 = wts[0, k, :, c * CHUNK : (c + 1) * CHUNK]
                w1 = wts[1, k, :, c * CHUNK : (c + 1) * CHUNK]
                left = jnp.concatenate([jnp.where(high == jnp.bfloat16(h), w0, zero) for h in range(LEVELS)], axis=0)
                rights = []
                for o in range(2):
                    eight = low[o * OCTET : (o + 1) * OCTET]
                    pair = (jnp.concatenate([eight, eight], axis=0) - upper).astype(jnp.float32).astype(jnp.bfloat16)
                    rights += [jnp.where(pair == jnp.bfloat16(l), w1, zero) for l in range(0, LEVELS, 2)]
                right = jnp.concatenate(rights, axis=0)
                part_sum = lax.dot_general(left, right, (((1,), (1,)), ((), ())), preferred_element_type=jnp.float32)
                side = index % 2
                sums[side] = part_sum if sums[side] is None else sums[side] + part_sum
                index += 1
        joint = sums[0] + sums[1]
        blocks = []
        for o in range(2):
            cut = slice(o * LANES, (o + 1) * LANES)
            rows = [joint[h * GROUP + o * OCTET : h * GROUP + (o + 1) * OCTET, cut] for h in range(LEVELS)]
            rows = [jnp.where(diagonal, r, 0.0) for r in rows]
            blocks.append(jnp.concatenate([gather_rows(rows[:8]), gather_rows(rows[8:])], axis=0))
        return blocks

    def shift_x(turn):
        return (2 + 3 * turn + 3 * (turn * (turn - 1) // 2)) % NX

    def target_of(step_x, step_y, o, far):
        return device((x + step_x) % NX, (z + far) % NZ, (y // 2 + step_y) % 2 * 2 + o, NC - 1)

    def outgoing(turn, half, o, far):
        target = target_of(shift_x(turn), 1 - half, o, far)
        return pltpu.make_async_remote_copy(
            src_ref=stage.at[2 * turn + half, o],
            dst_ref=inbox.at[(me - target + RANKS) % RANKS],
            send_sem=send_sem.at[0],
            recv_sem=recv_sem.at[0],
            device_id={"rows": target},
            device_id_type=MESH,
        )

    turns = STEPS // 2

    def do_pair(turn, carry):
        for half in range(2):
            group = (x + shift_x(turn)) % NX * 2 + (y // 2 + 1 - half) % 2
            for o, block in enumerate(group_hist(group)):
                stage[2 * turn + half, o] = block

        @pl.when(turn == 0)
        def _():
            pl.semaphore_wait(barrier, RANKS - 1)

        for far in (1, 0):
            for half in range(2):
                for o in range(2):
                    itself = owner & (turn == turns - 1) & (y % 2 == o) if half == 1 and far == 0 else None
                    if itself is None:
                        outgoing(turn, half, o, far).start()
                    else:
                        @pl.when(jnp.logical_not(itself))
                        def _():
                            outgoing(turn, half, o, far).start()

        return carry

    lax.fori_loop(0, turns, do_pair, 0)

    def spread(k):
        target = device((x + k // (NY * NC)) % NX, z, (y + k // NC % NY) % NY, (core + k % NC) % NC)
        return pltpu.make_async_remote_copy(
            src_ref=mine,
            dst_ref=out_ref.at[pl.ds(here, OCTET), :],
            send_sem=gather_send.at[0],
            recv_sem=gather_recv.at[0],
            device_id={"rows": target},
            device_id_type=MESH,
        )

    def drain(ref, sem):
        return pltpu.make_async_copy(ref, ref, sem.at[0])

    here = pl.multiple_of((x * NY + y) * OCTET, OCTET)

    @pl.when(owner)
    def _():
        drain(inbox.at[pl.ds(0, RANKS - 1)], recv_sem).wait()
        sums = [stage[STEPS - 1, y % 2], None, None, None]
        for s in range(1, RANKS):
            part = inbox[s]
            sums[s % 4] = part if sums[s % 4] is None else sums[s % 4] + part
        total = (sums[0] + sums[1]) + (sums[2] + sums[3])

        p0 = total.astype(jnp.bfloat16).astype(jnp.float32)
        p1 = (total - p0).astype(jnp.bfloat16).astype(jnp.float32)
        p2 = total - p0 - p1
        split = jnp.concatenate([p0, p1, p2], axis=0).astype(jnp.bfloat16)
        sums3 = jnp.dot(split, prefix[...], preferred_element_type=jnp.float32)
        joined = sums3[:LEVELS] + sums3[LEVELS : 2 * LEVELS] + sums3[2 * LEVELS :]
        inner, level = joined[:, :LANES], joined[:, LANES:]
        inv = 1.0 / (total + 1.0)
        whole = jnp.sum(level, axis=0, keepdims=True)
        target = column_ref[...] * whole
        run = jnp.zeros((1, LANES), jnp.float32)
        acc = jnp.zeros((thr_ref.shape[1], LANES), jnp.float32)
        for h in range(LEVELS):
            before = inner[h : h + 1] + run
            run = run + level[h : h + 1]
            ratio = (target - before) * inv[h : h + 1]
            acc = acc + jnp.clip(ratio, 0.0, 1.0)
        turned = acc.T
        cuts = turned[:OCTET]
        for j in range(1, LANES // OCTET):
            cuts = cuts + turned[j * OCTET : (j + 1) * OCTET]
        mine[...] = cuts
        for k in reversed(range(1, SEATS * NC)):
            spread(k).start()
        out_ref[pl.ds(here, OCTET), :] = cuts
        drain(inbox.at[pl.ds(0, 2 * SEATS - 1)], send_sem).wait()
        drain(out_ref.at[pl.ds(0, (SEATS - 1) * OCTET), :], gather_recv).wait()
        for k in range(1, SEATS * NC):
            spread(k).wait_send()

    @pl.when(jnp.logical_not(owner))
    def _():
        drain(inbox.at[pl.ds(0, 2 * SEATS)], send_sem).wait()
        drain(out_ref, gather_recv).wait()


def solution(mesh):
    def local(bins, hessian, thresholds):
        words, width = bins.shape
        quantiles = thresholds.shape[0]
        return pl.pallas_call(
            kernel,
            out_shape=pltpu.VMEM((width, quantiles), jnp.float32),
            in_specs=[pl.BlockSpec(memory_space=pl.ANY)] * 3,
            out_specs=pl.BlockSpec(memory_space=pltpu.VMEM),
            scratch_shapes=[
                pltpu.VMEM((words, width), jnp.int32),
                pltpu.VMEM((4 * words // LANES, LANES), jnp.float32),
                pltpu.VMEM((1, quantiles), jnp.float32),
                pltpu.VMEM((LANES, 2 * LANES), jnp.bfloat16),
                pltpu.VMEM((quantiles, LANES), jnp.float32),
                pltpu.VMEM((width, words), jnp.int32),
                pltpu.VMEM((2, 4, GROUP, words), jnp.bfloat16),
                pltpu.VMEM((STEPS, 2, LEVELS, LANES), jnp.float32),
                pltpu.VMEM((RANKS, LEVELS, LANES), jnp.float32),
                pltpu.VMEM((OCTET, quantiles), jnp.float32),
                pltpu.SemaphoreType.DMA((words // LANES + 2,)),
                pltpu.SemaphoreType.DMA((1,)),
                pltpu.SemaphoreType.DMA((1,)),
                pltpu.SemaphoreType.DMA((1,)),
                pltpu.SemaphoreType.DMA((1,)),
            ],
            compiler_params=pltpu.CompilerParams(collective_id=0, has_side_effects=True),
        )(bins, hessian.reshape(-1, LANES), thresholds.reshape(1, -1))

    in_specs = (P("rows", "feat"), P("rows"), P())
    return jax.shard_map(local, mesh=mesh, in_specs=in_specs, out_specs=P("feat", None), check_vma=False)
```

time: 42.1 us -> 26.6 us (0.63)
  the two profiles are of different devices: /device:TPU:33 before, /device:TPU:1 now
where the time goes in v1:
time: 26.6 us; the launch traced here: 26.5 us
  Pallas kernels  25.9 us (97%)
  local copies, waits for them, and re-layouts  0.63 us (2%)
    pallas_call x1, Pallas kernels, local(): pl.pallas_call(kernel, out_shape=pltpu.VMEM((width, quantiles), jnp.float...  25.9 us
    unnamed x1, local copies, waits for them, and re-layouts  0.63 us

profile of v1, /device:TPU:1, one launch (start us, length us, event | category | flops | bytes accessed | tf_op | source)
XLA Modules:
  0.0 26.5 jit_solution(159604314213009152)
XLA Ops:
  0.0 25.9 %shard_map.37 = f32[128,128]{1,0:T(8,128)S(1)} custom-call(s32[1024,128]{1,0:T(8,128)} %bins_hbm.1, f32[32,128]{1,0:T(8,128)} %bitcast.2, f32[1,128]{1,0:T(1,128)} %bitcast.3), custom_call_target="tpu_custom_call" | custom-call | tf_op jit(solution)/shard_map/pallas_call | solution.py:242
  25.9 0.6 %copy.5 = f32[128,128]{1,0:T(8,128)} copy(f32[128,128]{1,0:T(8,128)S(1)} %shard_map.37) | data formatting | bytes 131072

commit v2 on v1

--- a/solution.py
+++ b/solution.py
@@ -14,6 +14,8 @@
 RANKS = NX * NZ * NY * NC
 SEATS = NX * NY
 STEPS = SEATS // 2
+FRONT = 4
+SEND = 8
 MESH = pl.DeviceIdType.MESH
 
 
@@ -31,14 +33,17 @@
     thr_load.start()
     me = lax.axis_index("rows")
     x, z, y, core = me // (NZ * NY * NC), me // (NY * NC) % NZ, me // NC % NY, me % NC
-    owner = core == NC - 1
+    owner = (core == NC - 1) & (z == 0)
 
     def device(px, pz, py, pc):
         return ((px * NZ + pz) * NY + py) * NC + pc
 
     barrier = pltpu.get_barrier_semaphore()
-    for step in range(1, RANKS):
-        pl.semaphore_signal(barrier, inc=1, device_id={"rows": (me + step) % RANKS}, device_id_type=MESH)
+
+    @pl.when(owner)
+    def _():
+        for step in range(1, RANKS):
+            pl.semaphore_signal(barrier, inc=1, device_id={"rows": (me + step) % RANKS}, device_id_type=MESH)
 
     src = lax.broadcasted_iota(jnp.int32, (LANES, LANES), 0)
     dst = lax.broadcasted_iota(jnp.int32, (LANES, LANES), 1)
@@ -60,11 +65,16 @@
         away = jnp.abs(flat - other * factor)
         left_factor = jnp.where(away < miss, factor, left_factor)
         miss = jnp.minimum(miss, away)
+        if j == 63:
+            for t in range(tiles // 2):
+                bins_loads[t].wait()
+            for t in range(tiles // 2):
+                cols[:, t * LANES : (t + 1) * LANES] = bins_ref[t * LANES : (t + 1) * LANES, :].T
     right_factor = flat / left_factor
-    for t in range(tiles):
+    for t in range(tiles // 2, tiles):
         bins_loads[t].wait()
     thr_load.wait()
-    for t in range(tiles):
+    for t in range(tiles // 2, tiles):
         cols[:, t * LANES : (t + 1) * LANES] = bins_ref[t * LANES : (t + 1) * LANES, :].T
     column_ref[...] = jnp.broadcast_to(thr_ref[...], (LANES, thr_ref.shape[1])).T
     pieces = jnp.concatenate([x[j * tiles : (j + 1) * tiles] for j in range(4) for x in (left_factor, right_factor)], axis=0)
@@ -97,85 +107,98 @@
         p, q = two
         return jnp.where(low1, p, q) + jnp.where(low1, pltpu.roll(p, 7, 0), pltpu.roll(q, 1, 0))
 
-    def group_hist(group):
+    def products(group, first, last, sums):
         base = pl.multiple_of(group * GROUP, GROUP)
         zero = jnp.zeros((GROUP, CHUNK), jnp.bfloat16)
-        upper = (lax.broadcasted_iota(jnp.int32, (GROUP, CHUNK), 0) // OCTET)
-        sums = [None, None]
-        index = 0
-        for c in range(words // CHUNK):
+        upper = lax.broadcasted_iota(jnp.int32, (GROUP, CHUNK), 0) // OCTET
+        for index in range(first, last):
+            c, k = index // 4, index % 4
             part = cols[pl.ds(base, GROUP), c * CHUNK : (c + 1) * CHUNK]
-            for k in range(4):
-                high = jnp.bitwise_and(jnp.right_shift(part, 8 * k + 4), 15).astype(jnp.float32).astype(jnp.bfloat16)
-                low = jnp.bitwise_and(jnp.right_shift(part, 8 * k), 15)
-                w0 = wts[0, k, :, c * CHUNK : (c + 1) * CHUNK]
-                w1 = wts[1, k, :, c * CHUNK : (c + 1) * CHUNK]
-                left = jnp.concatenate([jnp.where(high == jnp.bfloat16(h), w0, zero) for h in range(LEVELS)], axis=0)
-                rights = []
-                for o in range(2):
-                    eight = low[o * OCTET : (o + 1) * OCTET]
-                    pair = (jnp.concatenate([eight, eight], axis=0) - upper).astype(jnp.float32).astype(jnp.bfloat16)
-                    rights += [jnp.where(pair == jnp.bfloat16(l), w1, zero) for l in range(0, LEVELS, 2)]
-                right = jnp.concatenate(rights, axis=0)
-                part_sum = lax.dot_general(left, right, (((1,), (1,)), ((), ())), preferred_element_type=jnp.float32)
-                side = index % 2
-                sums[side] = part_sum if sums[side] is None else sums[side] + part_sum
-                index += 1
-        joint = sums[0] + sums[1]
+            high = jnp.bitwise_and(jnp.right_shift(part, 8 * k + 4), 15).astype(jnp.float32).astype(jnp.bfloat16)
+            low = jnp.bitwise_and(jnp.right_shift(part, 8 * k), 15)
+            w0 = wts[0, k, :, c * CHUNK : (c + 1) * CHUNK]
+            w1 = wts[1, k, :, c * CHUNK : (c + 1) * CHUNK]
+            left = jnp.concatenate([jnp.where(high == jnp.bfloat16(h), w0, zero) for h in range(LEVELS)], axis=0)
+            rights = []
+            for o in range(2):
+                eight = low[o * OCTET : (o + 1) * OCTET]
+                pair = (jnp.concatenate([eight, eight], axis=0) - upper).astype(jnp.float32).astype(jnp.bfloat16)
+                rights += [jnp.where(pair == jnp.bfloat16(l), w1, zero) for l in range(0, LEVELS, 2)]
+            right = jnp.concatenate(rights, axis=0)
+            part_sum = lax.dot_general(left, right, (((1,), (1,)), ((), ())), preferred_element_type=jnp.float32)
+            side = index % 2
+            sums[side] = part_sum if sums[side] is None else sums[side] + part_sum
+
+    def extract(sums):
         blocks = []
         for o in range(2):
             cut = slice(o * LANES, (o + 1) * LANES)
-            rows = [joint[h * GROUP + o * OCTET : h * GROUP + (o + 1) * OCTET, cut] for h in range(LEVELS)]
-            rows = [jnp.where(diagonal, r, 0.0) for r in rows]
+            rows = []
+            for h in range(LEVELS):
+                pick = slice(h * GROUP + o * OCTET, h * GROUP + (o + 1) * OCTET)
+                rows.append(jnp.where(diagonal, sums[0][pick, cut], 0.0) + jnp.where(diagonal, sums[1][pick, cut], 0.0))
             blocks.append(jnp.concatenate([gather_rows(rows[:8]), gather_rows(rows[8:])], axis=0))
         return blocks
 
-    def shift_x(turn):
-        return (2 + 3 * turn + 3 * (turn * (turn - 1) // 2)) % NX
-
-    def target_of(step_x, step_y, o, far):
-        return device((x + step_x) % NX, (z + far) % NZ, (y // 2 + step_y) % 2 * 2 + o, NC - 1)
-
-    def outgoing(turn, half, o, far):
-        target = target_of(shift_x(turn), 1 - half, o, far)
+    place_x, place_y = (x + 1) % NX, (y + 1) % NY
+
+    def group_of(step):
+        block_x = (place_x // 2 + (1 if step < 4 else 0)) % 2
+        block_y = (place_y // 2 + (1 if step % 4 < 2 else 0)) % 2
+        return 2 * block_x + (place_x + 1 - step % 2) % 2, block_y
+
+    def outgoing(step, o):
+        column, block_y = group_of(step)
+        target = device((column + NX - 1) % NX, 0, (2 * block_y + o + NY - 1) % NY, NC - 1)
         return pltpu.make_async_remote_copy(
-            src_ref=stage.at[2 * turn + half, o],
-            dst_ref=inbox.at[(me - target + RANKS) % RANKS],
+            src_ref=stage.at[step, o],
+            dst_ref=inbox.at[step * OCTET + place_y % 2 * 4 + z * 2 + core],
             send_sem=send_sem.at[0],
-            recv_sem=recv_sem.at[0],
+            recv_sem=recv_sem.at[step // (STEPS - 1)],
             device_id={"rows": target},
             device_id_type=MESH,
         )
 
-    turns = STEPS // 2
-
-    def do_pair(turn, carry):
-        for half in range(2):
-            group = (x + shift_x(turn)) % NX * 2 + (y // 2 + 1 - half) % 2
-            for o, block in enumerate(group_hist(group)):
-                stage[2 * turn + half, o] = block
-
-        @pl.when(turn == 0)
-        def _():
-            pl.semaphore_wait(barrier, RANKS - 1)
-
-        for far in (1, 0):
-            for half in range(2):
-                for o in range(2):
-                    itself = owner & (turn == turns - 1) & (y % 2 == o) if half == 1 and far == 0 else None
-                    if itself is None:
-                        outgoing(turn, half, o, far).start()
-                    else:
-                        @pl.when(jnp.logical_not(itself))
-                        def _():
-                            outgoing(turn, half, o, far).start()
-
-        return carry
-
-    lax.fori_loop(0, turns, do_pair, 0)
-
-    def spread(k):
-        target = device((x + k // (NY * NC)) % NX, z, (y + k // NC % NY) % NY, (core + k % NC) % NC)
+    pl.semaphore_wait(barrier, SEATS - owner.astype(jnp.int32))
+    pieces_all = words // CHUNK * 4
+
+    def keep(step, sums):
+        for o, block in enumerate(extract(sums)):
+            stage[step, o] = block
+
+    def send(step):
+        for o in range(2):
+            if step < STEPS - 1:
+                outgoing(step, o).start()
+            else:
+
+                own = owner & (place_y % 2 == o)
+
+                @pl.when(own)
+                def _():
+                    inbox[step * OCTET + o * 4 + core] = stage[step, o]
+
+                @pl.when(jnp.logical_not(own))
+                def _():
+                    outgoing(step, o).start()
+
+    before_sums = None
+    for step in range(STEPS):
+        column, block_y = group_of(step)
+        group = column * 2 + block_y
+        sums = [None, None]
+        products(group, 0, FRONT, sums)
+        if step > 0:
+            keep(step - 1, before_sums)
+        products(group, FRONT, SEND, sums)
+        if step > 0:
+            send(step - 1)
+        products(group, SEND, pieces_all, sums)
+        before_sums = sums
+    keep(STEPS - 1, before_sums)
+    send(STEPS - 1)
+
+    def spread(target):
         return pltpu.make_async_remote_copy(
             src_ref=mine,
             dst_ref=out_ref.at[pl.ds(here, OCTET), :],
@@ -185,18 +208,33 @@
             device_id_type=MESH,
         )
 
+    def spread_owners():
+        first = (NX - x) % NX * NY + (NY - y) % NY
+        for k in range(SEATS - 1):
+            shift = (first + k) % SEATS
+            shift = shift + (1 - (shift + SEATS - 1) // SEATS) * ((first + SEATS - 1) % SEATS)
+            yield spread(device((x + shift // NY) % NX, 0, (y + shift % NY) % NY, NC - 1))
+
+    def spread_chip(px, py):
+        for pz, pc in ((1, 1), (1, 0), (0, 0)):
+            yield spread(device(px, pz, py, pc))
+
     def drain(ref, sem):
-        return pltpu.make_async_copy(ref, ref, sem.at[0])
-
-    here = pl.multiple_of((x * NY + y) * OCTET, OCTET)
+        return pltpu.make_async_copy(ref, ref, sem)
+
+    here = pl.multiple_of((place_x * NY + place_y) * OCTET, OCTET)
+    late = (0, 1, 2, 2)
+    chips = sorted(((px, py) for px in range(NX) for py in range(NY)), key=lambda c: late[c[0]] + late[c[1]])
 
     @pl.when(owner)
     def _():
-        drain(inbox.at[pl.ds(0, RANKS - 1)], recv_sem).wait()
-        sums = [stage[STEPS - 1, y % 2], None, None, None]
-        for s in range(1, RANKS):
-            part = inbox[s]
-            sums[s % 4] = part if sums[s % 4] is None else sums[s % 4] + part
+        drain(inbox.at[pl.ds(0, RANKS - OCTET)], recv_sem.at[0]).wait()
+        sums = [None] * 4
+        for s in range(RANKS - OCTET):
+            sums[s % 4] = inbox[s] if sums[s % 4] is None else sums[s % 4] + inbox[s]
+        drain(inbox.at[pl.ds(0, OCTET - 1)], recv_sem.at[1]).wait()
+        for s in range(RANKS - OCTET, RANKS):
+            sums[s % 4] = sums[s % 4] + inbox[s]
         total = (sums[0] + sums[1]) + (sums[2] + sums[3])
 
         p0 = total.astype(jnp.bfloat16).astype(jnp.float32)
@@ -221,18 +259,21 @@
         for j in range(1, LANES // OCTET):
             cuts = cuts + turned[j * OCTET : (j + 1) * OCTET]
         mine[...] = cuts
-        for k in reversed(range(1, SEATS * NC)):
-            spread(k).start()
+        owners = list(spread_owners())
+        others = [copy for px, py in chips for copy in spread_chip(px, py)]
+        copies = owners[:1] + others[:18] + owners[1:] + others[18:]
+        for copy in copies:
+            copy.start()
         out_ref[pl.ds(here, OCTET), :] = cuts
-        drain(inbox.at[pl.ds(0, 2 * SEATS - 1)], send_sem).wait()
-        drain(out_ref.at[pl.ds(0, (SEATS - 1) * OCTET), :], gather_recv).wait()
-        for k in range(1, SEATS * NC):
-            spread(k).wait_send()
+        drain(inbox.at[pl.ds(0, SEATS - 1)], send_sem.at[0]).wait()
+        drain(out_ref.at[pl.ds(0, (SEATS - 1) * OCTET), :], gather_recv.at[0]).wait()
+        for copy in copies:
+            copy.wait_send()
 
     @pl.when(jnp.logical_not(owner))
     def _():
-        drain(inbox.at[pl.ds(0, 2 * SEATS)], send_sem).wait()
-        drain(out_ref, gather_recv).wait()
+        drain(inbox.at[pl.ds(0, SEATS)], send_sem.at[0]).wait()
+        drain(out_ref, gather_recv.at[0]).wait()
 
 
 def solution(mesh):
@@ -257,7 +298,7 @@
                 pltpu.VMEM((OCTET, quantiles), jnp.float32),
                 pltpu.SemaphoreType.DMA((words // LANES + 2,)),
                 pltpu.SemaphoreType.DMA((1,)),
-                pltpu.SemaphoreType.DMA((1,)),
+                pltpu.SemaphoreType.DMA((2,)),
                 pltpu.SemaphoreType.DMA((1,)),
                 pltpu.SemaphoreType.DMA((1,)),
             ],

time: 26.6 us -> 24.6 us (0.925); the launches traced: 26.5 us -> 24.1 us
  Pallas kernels: 25.9 us -> 23.5 us
    pallas_call x1, Pallas kernels: 25.9 us -> 23.5 us  [local(): pl.pallas_call(kernel, out_shape=pltpu.VMEM((width, quantiles), jnp.float...]
where the time goes in v2:
time: 24.6 us; the launch traced here: 24.1 us
  Pallas kernels  23.5 us (96%)
  local copies, waits for them, and re-layouts  0.63 us (3%)
    pallas_call x1, Pallas kernels, local(): pl.pallas_call(kernel, out_shape=pltpu.VMEM((width, quantiles), jnp.float...  23.5 us
    unnamed x1, local copies, waits for them, and re-layouts  0.63 us

profile of v2, /device:TPU:1, one launch (start us, length us, event | category | flops | bytes accessed | tf_op | source)
XLA Modules:
  0.0 24.1 jit_solution(11494863335659067405)
XLA Ops:
  0.0 23.5 %shard_map.37 = f32[128,128]{1,0:T(8,128)S(1)} custom-call(s32[1024,128]{1,0:T(8,128)} %bins_hbm.1, f32[32,128]{1,0:T(8,128)} %bitcast.2, f32[1,128]{1,0:T(1,128)} %bitcast.3), custom_call_target="tpu_custom_call" | custom-call | tf_op jit(solution)/shard_map/pallas_call | solution.py:283
  23.5 0.6 %copy.5 = f32[128,128]{1,0:T(8,128)} copy(f32[128,128]{1,0:T(8,128)S(1)} %shard_map.37) | data formatting | bytes 131072

commit v3 on v2

--- a/solution.py
+++ b/solution.py
@@ -13,13 +13,23 @@
 NX, NZ, NY, NC = 4, 2, 4, 2
 RANKS = NX * NZ * NY * NC
 SEATS = NX * NY
-STEPS = SEATS // 2
+STEPS = 4
 FRONT = 4
 SEND = 8
+MEET = 8
+SLOTS = STEPS * OCTET
 MESH = pl.DeviceIdType.MESH
 
 
-def kernel(bins_hbm, hess_hbm, thr_hbm, out_ref, bins_ref, hess_ref, thr_ref, prefix, column_ref, cols, wts, stage, inbox, mine, load_sem, send_sem, recv_sem, gather_send, gather_recv):
+def mod(value, size):
+    return lax.rem(value, jnp.int32(size)) if isinstance(value, jax.Array) else value % size
+
+
+def div(value, size):
+    return lax.div(value, jnp.int32(size)) if isinstance(value, jax.Array) else value // size
+
+
+def kernel(bins_hbm, hess_hbm, thr_hbm, out_ref, bins_ref, hess_ref, thr_ref, prefix, column_ref, cols, wts, lines, other_cols, other_wts, other_lines, partial, stage, inbox, mine, load_sem, swap_send, swap_recv, send_sem, recv_sem, gather_send, gather_recv, hello, go):
     words, width = bins_ref.shape
     tiles = words // LANES
     hess_load = pltpu.make_async_copy(hess_hbm, hess_ref, load_sem.at[tiles])
@@ -32,18 +42,28 @@
     thr_load = pltpu.make_async_copy(thr_hbm, thr_ref, load_sem.at[tiles + 1])
     thr_load.start()
     me = lax.axis_index("rows")
-    x, z, y, core = me // (NZ * NY * NC), me // (NY * NC) % NZ, me // NC % NY, me % NC
+    x, z, y, core = div(me, NZ * NY * NC), mod(div(me, NY * NC), NZ), mod(div(me, NC), NY), mod(me, NC)
     owner = (core == NC - 1) & (z == 0)
 
     def device(px, pz, py, pc):
         return ((px * NZ + pz) * NY + py) * NC + pc
 
+    partner = device(x, z, y, 1 - core)
     barrier = pltpu.get_barrier_semaphore()
 
+    @pl.when(core == 1)
+    def _():
+        pl.semaphore_signal(barrier, inc=1, device_id={"rows": partner}, device_id_type=MESH)
+
     @pl.when(owner)
     def _():
-        for step in range(1, RANKS):
-            pl.semaphore_signal(barrier, inc=1, device_id={"rows": (me + step) % RANKS}, device_id_type=MESH)
+        for step in range(NC, RANKS, NC):
+            pl.semaphore_signal(barrier, inc=1, device_id={"rows": mod(me + step, RANKS)}, device_id_type=MESH)
+
+    @pl.when(core == 0)
+    def _():
+        pl.semaphore_wait(barrier, 1)
+        pl.semaphore_signal(hello, inc=1, device_id={"rows": partner}, device_id_type=MESH)
 
     src = lax.broadcasted_iota(jnp.int32, (LANES, LANES), 0)
     dst = lax.broadcasted_iota(jnp.int32, (LANES, LANES), 1)
@@ -86,10 +106,40 @@
             if j != k:
                 block = pltpu.roll(block, (quarter * (j - k)) % LANES, 1)
             plane = block if plane is None else jnp.where(lane == j, block, plane)
-        for piece in range(2):
-            for t in range(tiles):
-                line = plane[piece * tiles + t : piece * tiles + t + 1]
-                wts[piece, k, :, t * LANES : (t + 1) * LANES] = jnp.broadcast_to(line, (GROUP, LANES)).astype(jnp.bfloat16)
+        lines[k] = plane
+
+    def widen(target, source):
+        for k in range(4):
+            plane = source[k]
+            for piece in range(2):
+                for t in range(tiles):
+                    line = plane[piece * tiles + t : piece * tiles + t + 1]
+                    target[piece, k, :, t * LANES : (t + 1) * LANES] = jnp.broadcast_to(line, (GROUP, LANES)).astype(jnp.bfloat16)
+
+    half = width // 4
+
+    def swap(piece):
+        if piece < 2:
+            there = pl.multiple_of(piece * 2 * half + (1 - core) * half, half)
+            source, target = cols.at[pl.ds(there, half), :], other_cols.at[pl.ds(piece * half, half), :]
+        else:
+            source, target = lines, other_lines
+        return pltpu.make_async_remote_copy(
+            src_ref=source,
+            dst_ref=target,
+            send_sem=swap_send.at[piece],
+            recv_sem=swap_recv.at[piece],
+            device_id={"rows": partner},
+            device_id_type=MESH,
+        )
+
+    @pl.when(core == 1)
+    def _():
+        pl.semaphore_wait(hello, 1)
+
+    for piece in (2, 0, 1):
+        swap(piece).start()
+    widen(wts, lines)
 
     sub = lax.broadcasted_iota(jnp.int32, (OCTET, LANES), 0)
     diagonal = sub == lax.broadcasted_iota(jnp.int32, (OCTET, LANES), 1) % OCTET
@@ -107,17 +157,16 @@
         p, q = two
         return jnp.where(low1, p, q) + jnp.where(low1, pltpu.roll(p, 7, 0), pltpu.roll(q, 1, 0))
 
-    def products(group, first, last, sums):
-        base = pl.multiple_of(group * GROUP, GROUP)
+    def products(columns, weights, base, first, last, sums):
         zero = jnp.zeros((GROUP, CHUNK), jnp.bfloat16)
         upper = lax.broadcasted_iota(jnp.int32, (GROUP, CHUNK), 0) // OCTET
         for index in range(first, last):
             c, k = index // 4, index % 4
-            part = cols[pl.ds(base, GROUP), c * CHUNK : (c + 1) * CHUNK]
+            part = columns[pl.ds(base, GROUP), c * CHUNK : (c + 1) * CHUNK]
             high = jnp.bitwise_and(jnp.right_shift(part, 8 * k + 4), 15).astype(jnp.float32).astype(jnp.bfloat16)
             low = jnp.bitwise_and(jnp.right_shift(part, 8 * k), 15)
-            w0 = wts[0, k, :, c * CHUNK : (c + 1) * CHUNK]
-            w1 = wts[1, k, :, c * CHUNK : (c + 1) * CHUNK]
+            w0 = weights[0, k, :, c * CHUNK : (c + 1) * CHUNK]
+            w1 = weights[1, k, :, c * CHUNK : (c + 1) * CHUNK]
             left = jnp.concatenate([jnp.where(high == jnp.bfloat16(h), w0, zero) for h in range(LEVELS)], axis=0)
             rights = []
             for o in range(2):
@@ -137,65 +186,92 @@
             for h in range(LEVELS):
                 pick = slice(h * GROUP + o * OCTET, h * GROUP + (o + 1) * OCTET)
                 rows.append(jnp.where(diagonal, sums[0][pick, cut], 0.0) + jnp.where(diagonal, sums[1][pick, cut], 0.0))
-            blocks.append(jnp.concatenate([gather_rows(rows[:8]), gather_rows(rows[8:])], axis=0))
+            blocks.append([gather_rows(rows[:8]), gather_rows(rows[8:])])
         return blocks
 
-    place_x, place_y = (x + 1) % NX, (y + 1) % NY
-
-    def group_of(step):
-        block_x = (place_x // 2 + (1 if step < 4 else 0)) % 2
-        block_y = (place_y // 2 + (1 if step % 4 < 2 else 0)) % 2
-        return 2 * block_x + (place_x + 1 - step % 2) % 2, block_y
+    place_x, place_y = mod(x + 1, NX), mod(y + 1, NY)
+
+    def block_of(step):
+        return mod(div(place_x, 2) + (1 if step < 2 else 0), 2), mod(div(place_y, 2) + (1 if step % 2 == 0 else 0), 2)
 
     def outgoing(step, o):
-        column, block_y = group_of(step)
-        target = device((column + NX - 1) % NX, 0, (2 * block_y + o + NY - 1) % NY, NC - 1)
+        block_x, block_y = block_of(step)
+        target = device(mod(2 * block_x + core + NX - 1, NX), 0, mod(2 * block_y + o + NY - 1, NY), NC - 1)
         return pltpu.make_async_remote_copy(
             src_ref=stage.at[step, o],
-            dst_ref=inbox.at[step * OCTET + place_y % 2 * 4 + z * 2 + core],
+            dst_ref=inbox.at[pl.ds(2 * (step * OCTET + mod(place_x, 2) * 4 + mod(place_y, 2) * 2 + z), 2)],
             send_sem=send_sem.at[0],
             recv_sem=recv_sem.at[step // (STEPS - 1)],
             device_id={"rows": target},
             device_id_type=MESH,
         )
 
-    pl.semaphore_wait(barrier, SEATS - owner.astype(jnp.int32))
     pieces_all = words // CHUNK * 4
-
-    def keep(step, sums):
+    keeps = owner & (mod(place_x, 2) == core)
+
+    def keep(step, theirs, alone, sums):
         for o, block in enumerate(extract(sums)):
-            stage[step, o] = block
+            for part in range(2):
+                if not theirs:
+                    partial[step, o, part] = block[part]
+                else:
+                    stage[step, o, part] = block[part] if alone else block[part] + partial[step, o, part]
 
     def send(step):
         for o in range(2):
             if step < STEPS - 1:
                 outgoing(step, o).start()
             else:
-
-                own = owner & (place_y % 2 == o)
+                own = keeps & (mod(place_y, 2) == o)
 
                 @pl.when(own)
                 def _():
-                    inbox[step * OCTET + o * 4 + core] = stage[step, o]
+                    inbox[pl.ds(2 * (step * OCTET + mod(place_x, 2) * 4 + o * 2), 2)] = stage[step, o]
 
                 @pl.when(jnp.logical_not(own))
                 def _():
                     outgoing(step, o).start()
 
-    before_sums = None
-    for step in range(STEPS):
-        column, block_y = group_of(step)
-        group = column * 2 + block_y
+    def span(step, theirs, first, last, sums):
+        block_x, block_y = block_of(step)
+        if theirs:
+            base = pl.multiple_of(block_x * half + block_y * GROUP, GROUP)
+            products(other_cols, other_wts, base, first, last, sums)
+        else:
+            base = pl.multiple_of((2 * block_x + core) * half + block_y * GROUP, GROUP)
+            products(cols, wts, base, first, last, sums)
+
+    parts = [(step, theirs) for theirs in (False, True) for step in range(STEPS - 1)] + [(STEPS - 1, False)]
+    last = None
+    for index, (step, theirs) in enumerate(parts):
         sums = [None, None]
-        products(group, 0, FRONT, sums)
-        if step > 0:
-            keep(step - 1, before_sums)
-        products(group, FRONT, SEND, sums)
-        if step > 0:
-            send(step - 1)
-        products(group, SEND, pieces_all, sums)
-        before_sums = sums
-    keep(STEPS - 1, before_sums)
+        span(step, theirs, 0, FRONT, sums)
+        if last is not None:
+            keep(*last)
+        span(step, theirs, FRONT, SEND, sums)
+        if last is not None and last[1]:
+            if last[0] == 0:
+                @pl.when(core == 1)
+                def _():
+                    pl.semaphore_wait(barrier, SEATS - owner.astype(jnp.int32))
+                    pl.semaphore_signal(go, inc=1, device_id={"rows": partner}, device_id_type=MESH)
+
+                @pl.when(core == 0)
+                def _():
+                    pl.semaphore_wait(go, 1)
+
+            send(last[0])
+        if index == STEPS - 2:
+            span(step, theirs, SEND, MEET, sums)
+            for piece in range(3):
+                swap(piece).wait()
+            widen(other_wts, other_lines)
+            span(step, theirs, MEET, pieces_all, sums)
+        else:
+            span(step, theirs, SEND, pieces_all, sums)
+        last = step, theirs, False, sums
+    span(STEPS - 1, True, 0, pieces_all, sums)
+    keep(STEPS - 1, True, True, sums)
     send(STEPS - 1)
 
     def spread(target):
@@ -209,11 +285,11 @@
         )
 
     def spread_owners():
-        first = (NX - x) % NX * NY + (NY - y) % NY
+        first = mod(NX - x, NX) * NY + mod(NY - y, NY)
         for k in range(SEATS - 1):
-            shift = (first + k) % SEATS
-            shift = shift + (1 - (shift + SEATS - 1) // SEATS) * ((first + SEATS - 1) % SEATS)
-            yield spread(device((x + shift // NY) % NX, 0, (y + shift % NY) % NY, NC - 1))
+            shift = mod(first + k, SEATS)
+            shift = shift + (1 - div(shift + SEATS - 1, SEATS)) * mod(first + SEATS - 1, SEATS)
+            yield spread(device(mod(x + div(shift, NY), NX), 0, mod(y + mod(shift, NY), NY), NC - 1))
 
     def spread_chip(px, py):
         for pz, pc in ((1, 1), (1, 0), (0, 0)):
@@ -226,16 +302,32 @@
     late = (0, 1, 2, 2)
     chips = sorted(((px, py) for px in range(NX) for py in range(NY)), key=lambda c: late[c[0]] + late[c[1]])
 
+    @pl.when(keeps)
+    def _():
+        drain(inbox.at[pl.ds(0, 2 * (2 * STEPS - 1))], send_sem.at[0]).wait()
+
+    @pl.when(jnp.logical_not(keeps))
+    def _():
+        drain(inbox.at[pl.ds(0, 4 * STEPS)], send_sem.at[0]).wait()
+
     @pl.when(owner)
     def _():
-        drain(inbox.at[pl.ds(0, RANKS - OCTET)], recv_sem.at[0]).wait()
+        drain(inbox.at[pl.ds(0, 2 * (SLOTS - OCTET))], recv_sem.at[0]).wait()
         sums = [None] * 4
-        for s in range(RANKS - OCTET):
+        for s in range(2 * (SLOTS - OCTET)):
             sums[s % 4] = inbox[s] if sums[s % 4] is None else sums[s % 4] + inbox[s]
-        drain(inbox.at[pl.ds(0, OCTET - 1)], recv_sem.at[1]).wait()
-        for s in range(RANKS - OCTET, RANKS):
+
+        @pl.when(keeps)
+        def _():
+            drain(inbox.at[pl.ds(0, 2 * (OCTET - 1))], recv_sem.at[1]).wait()
+
+        @pl.when(jnp.logical_not(keeps))
+        def _():
+            drain(inbox.at[pl.ds(0, 2 * OCTET)], recv_sem.at[1]).wait()
+
+        for s in range(2 * (SLOTS - OCTET), 2 * SLOTS):
             sums[s % 4] = sums[s % 4] + inbox[s]
-        total = (sums[0] + sums[1]) + (sums[2] + sums[3])
+        total = jnp.concatenate([sums[0] + sums[2], sums[1] + sums[3]], axis=0)
 
         p0 = total.astype(jnp.bfloat16).astype(jnp.float32)
         p1 = (total - p0).astype(jnp.bfloat16).astype(jnp.float32)
@@ -265,14 +357,11 @@
         for copy in copies:
             copy.start()
         out_ref[pl.ds(here, OCTET), :] = cuts
-        drain(inbox.at[pl.ds(0, SEATS - 1)], send_sem.at[0]).wait()
+        drain(inbox.at[pl.ds(0, RANKS - 1)], gather_send.at[0]).wait()
         drain(out_ref.at[pl.ds(0, (SEATS - 1) * OCTET), :], gather_recv.at[0]).wait()
-        for copy in copies:
-            copy.wait_send()
 
     @pl.when(jnp.logical_not(owner))
     def _():
-        drain(inbox.at[pl.ds(0, SEATS)], send_sem.at[0]).wait()
         drain(out_ref, gather_recv.at[0]).wait()
 
 
@@ -293,14 +382,23 @@
                 pltpu.VMEM((quantiles, LANES), jnp.float32),
                 pltpu.VMEM((width, words), jnp.int32),
                 pltpu.VMEM((2, 4, GROUP, words), jnp.bfloat16),
-                pltpu.VMEM((STEPS, 2, LEVELS, LANES), jnp.float32),
-                pltpu.VMEM((RANKS, LEVELS, LANES), jnp.float32),
+                pltpu.VMEM((4, 2 * words // LANES, LANES), jnp.float32),
+                pltpu.VMEM((width // 2, words), jnp.int32),
+                pltpu.VMEM((2, 4, GROUP, words), jnp.bfloat16),
+                pltpu.VMEM((4, 2 * words // LANES, LANES), jnp.float32),
+                pltpu.VMEM((STEPS, 2, 2, OCTET, LANES), jnp.float32),
+                pltpu.VMEM((STEPS, 2, 2, OCTET, LANES), jnp.float32),
+                pltpu.VMEM((2 * SLOTS, OCTET, LANES), jnp.float32),
                 pltpu.VMEM((OCTET, quantiles), jnp.float32),
                 pltpu.SemaphoreType.DMA((words // LANES + 2,)),
+                pltpu.SemaphoreType.DMA((3,)),
+                pltpu.SemaphoreType.DMA((3,)),
                 pltpu.SemaphoreType.DMA((1,)),
                 pltpu.SemaphoreType.DMA((2,)),
                 pltpu.SemaphoreType.DMA((1,)),
                 pltpu.SemaphoreType.DMA((1,)),
+                pltpu.SemaphoreType.REGULAR,
+                pltpu.SemaphoreType.REGULAR,
             ],
             compiler_params=pltpu.CompilerParams(collective_id=0, has_side_effects=True),
         )(bins, hessian.reshape(-1, LANES), thresholds.reshape(1, -1))

time: 24.6 us -> 23.5 us (0.955); the launches traced: 24.1 us -> 23.4 us
  Pallas kernels: 23.5 us -> 22.7 us
    pallas_call x1, Pallas kernels: 23.5 us -> 22.7 us  [local(): pl.pallas_call(kernel, out_shape=pltpu.VMEM((width, quantiles), jnp.float...]
where the time goes in v3:
time: 23.5 us; the launch traced here: 23.4 us
  Pallas kernels  22.7 us (97%)
  local copies, waits for them, and re-layouts  0.63 us (3%)
    pallas_call x1, Pallas kernels, local(): pl.pallas_call(kernel, out_shape=pltpu.VMEM((width, quantiles), jnp.float...  22.7 us
    unnamed x1, local copies, waits for them, and re-layouts  0.63 us

profile of v3, /device:TPU:1, one launch (start us, length us, event | category | flops | bytes accessed | tf_op | source)
XLA Modules:
  0.0 23.4 jit_solution(3405028121423201026)
XLA Ops:
  0.0 22.7 %shard_map.37 = f32[128,128]{1,0:T(8,128)S(1)} custom-call(s32[1024,128]{1,0:T(8,128)} %bins_hbm.1, f32[32,128]{1,0:T(8,128)} %bitcast.2, f32[1,128]{1,0:T(1,128)} %bitcast.3), custom_call_target="tpu_custom_call" | custom-call | tf_op jit(solution)/shard_map/pallas_call | solution.py:372
  22.8 0.6 %copy.5 = f32[128,128]{1,0:T(8,128)} copy(f32[128,128]{1,0:T(8,128)S(1)} %shard_map.37) | data formatting | bytes 131072

commit v4 on v3

--- a/solution.py
+++ b/solution.py
@@ -251,11 +251,6 @@
         span(step, theirs, FRONT, SEND, sums)
         if last is not None and last[1]:
             if last[0] == 0:
-                @pl.when(core == 1)
-                def _():
-                    pl.semaphore_wait(barrier, SEATS - owner.astype(jnp.int32))
-                    pl.semaphore_signal(go, inc=1, device_id={"rows": partner}, device_id_type=MESH)
-
                 @pl.when(core == 0)
                 def _():
                     pl.semaphore_wait(go, 1)
@@ -263,6 +258,12 @@
             send(last[0])
         if index == STEPS - 2:
             span(step, theirs, SEND, MEET, sums)
+
+            @pl.when(core == 1)
+            def _():
+                pl.semaphore_wait(barrier, SEATS - owner.astype(jnp.int32))
+                pl.semaphore_signal(go, inc=1, device_id={"rows": partner}, device_id_type=MESH)
+
             for piece in range(3):
                 swap(piece).wait()
             widen(other_wts, other_lines)

time: 23.5 us -> 23.5 us (level)
  no operation moved by 1% of the time
where the time goes in v4:
time: 23.5 us; the launch traced here: 23.4 us
  Pallas kernels  22.7 us (97%)
  local copies, waits for them, and re-layouts  0.63 us (3%)
    pallas_call x1, Pallas kernels, local(): pl.pallas_call(kernel, out_shape=pltpu.VMEM((width, quantiles), jnp.float...  22.7 us
    unnamed x1, local copies, waits for them, and re-layouts  0.63 us

profile of v4, /device:TPU:1, one launch (start us, length us, event | category | flops | bytes accessed | tf_op | source)
XLA Modules:
  0.0 23.4 jit_solution(4632721814462417011)
XLA Ops:
  0.0 22.7 %shard_map.37 = f32[128,128]{1,0:T(8,128)S(1)} custom-call(s32[1024,128]{1,0:T(8,128)} %bins_hbm.1, f32[32,128]{1,0:T(8,128)} %bitcast.2, f32[1,128]{1,0:T(1,128)} %bitcast.3), custom_call_target="tpu_custom_call" | custom-call | tf_op jit(solution)/shard_map/pallas_call | solution.py:373
  22.7 0.6 %copy.5 = f32[128,128]{1,0:T(8,128)} copy(f32[128,128]{1,0:T(8,128)S(1)} %shard_map.37) | data formatting | bytes 131072

commit v5 on v4

--- a/solution.py
+++ b/solution.py
@@ -96,26 +96,6 @@
     thr_load.wait()
     for t in range(tiles // 2, tiles):
         cols[:, t * LANES : (t + 1) * LANES] = bins_ref[t * LANES : (t + 1) * LANES, :].T
-    column_ref[...] = jnp.broadcast_to(thr_ref[...], (LANES, thr_ref.shape[1])).T
-    pieces = jnp.concatenate([x[j * tiles : (j + 1) * tiles] for j in range(4) for x in (left_factor, right_factor)], axis=0)
-    moved = jnp.dot(pieces.astype(jnp.bfloat16), order, preferred_element_type=jnp.float32)
-    for k in range(4):
-        plane = None
-        for j in range(4):
-            block = moved[2 * tiles * j : 2 * tiles * (j + 1)]
-            if j != k:
-                block = pltpu.roll(block, (quarter * (j - k)) % LANES, 1)
-            plane = block if plane is None else jnp.where(lane == j, block, plane)
-        lines[k] = plane
-
-    def widen(target, source):
-        for k in range(4):
-            plane = source[k]
-            for piece in range(2):
-                for t in range(tiles):
-                    line = plane[piece * tiles + t : piece * tiles + t + 1]
-                    target[piece, k, :, t * LANES : (t + 1) * LANES] = jnp.broadcast_to(line, (GROUP, LANES)).astype(jnp.bfloat16)
-
     half = width // 4
 
     def swap(piece):
@@ -137,9 +117,32 @@
     def _():
         pl.semaphore_wait(hello, 1)
 
-    for piece in (2, 0, 1):
+    for piece in range(2):
         swap(piece).start()
-    widen(wts, lines)
+    column_ref[...] = jnp.broadcast_to(thr_ref[...], (LANES, thr_ref.shape[1])).T
+    pieces = jnp.concatenate([x[j * tiles : (j + 1) * tiles] for j in range(4) for x in (left_factor, right_factor)], axis=0)
+    moved = jnp.dot(pieces.astype(jnp.bfloat16), order, preferred_element_type=jnp.float32)
+    planes = []
+    for k in range(4):
+        plane = None
+        for j in range(4):
+            block = moved[2 * tiles * j : 2 * tiles * (j + 1)]
+            if j != k:
+                block = pltpu.roll(block, (quarter * (j - k)) % LANES, 1)
+            plane = block if plane is None else jnp.where(lane == j, block, plane)
+        lines[k] = plane
+        planes.append(plane)
+
+    def widen(target, source):
+        for k in range(4):
+            plane = source[k]
+            for piece in range(2):
+                for t in range(tiles):
+                    line = plane[piece * tiles + t : piece * tiles + t + 1]
+                    target[piece, k, :, t * LANES : (t + 1) * LANES] = jnp.broadcast_to(line, (GROUP, LANES)).astype(jnp.bfloat16)
+
+    swap(2).start()
+    widen(wts, planes)
 
     sub = lax.broadcasted_iota(jnp.int32, (OCTET, LANES), 0)
     diagonal = sub == lax.broadcasted_iota(jnp.int32, (OCTET, LANES), 1) % OCTET

time: 23.5 us -> 23.6 us (level)
  no operation moved by 1% of the time
where the time goes in v5:
time: 23.6 us; the launch traced here: 23.4 us
  Pallas kernels  22.8 us (97%)
  local copies, waits for them, and re-layouts  0.63 us (3%)
    pallas_call x1, Pallas kernels, local(): pl.pallas_call(kernel, out_shape=pltpu.VMEM((width, quantiles), jnp.float...  22.8 us
    unnamed x1, local copies, waits for them, and re-layouts  0.63 us

profile of v5, /device:TPU:1, one launch (start us, length us, event | category | flops | bytes accessed | tf_op | source)
XLA Modules:
  0.0 23.4 jit_solution(17495268045579321911)
XLA Ops:
  0.0 22.8 %shard_map.37 = f32[128,128]{1,0:T(8,128)S(1)} custom-call(s32[1024,128]{1,0:T(8,128)} %bins_hbm.1, f32[32,128]{1,0:T(8,128)} %bitcast.2, f32[1,128]{1,0:T(1,128)} %bitcast.3), custom_call_target="tpu_custom_call" | custom-call | tf_op jit(solution)/shard_map/pallas_call | solution.py:376
  22.8 0.6 %copy.5 = f32[128,128]{1,0:T(8,128)} copy(f32[128,128]{1,0:T(8,128)S(1)} %shard_map.37) | data formatting | bytes 131072

commit v6 on v4

--- a/solution.py
+++ b/solution.py
@@ -99,6 +99,7 @@
     column_ref[...] = jnp.broadcast_to(thr_ref[...], (LANES, thr_ref.shape[1])).T
     pieces = jnp.concatenate([x[j * tiles : (j + 1) * tiles] for j in range(4) for x in (left_factor, right_factor)], axis=0)
     moved = jnp.dot(pieces.astype(jnp.bfloat16), order, preferred_element_type=jnp.float32)
+    planes = []
     for k in range(4):
         plane = None
         for j in range(4):
@@ -107,6 +108,7 @@
                 block = pltpu.roll(block, (quarter * (j - k)) % LANES, 1)
             plane = block if plane is None else jnp.where(lane == j, block, plane)
         lines[k] = plane
+        planes.append(plane)
 
     def widen(target, source):
         for k in range(4):
@@ -139,7 +141,7 @@
 
     for piece in (2, 0, 1):
         swap(piece).start()
-    widen(wts, lines)
+    widen(wts, planes)
 
     sub = lax.broadcasted_iota(jnp.int32, (OCTET, LANES), 0)
     diagonal = sub == lax.broadcasted_iota(jnp.int32, (OCTET, LANES), 1) % OCTET

time: 23.5 us -> 23.5 us (level)
  no operation moved by 1% of the time
where the time goes in v6:
time: 23.5 us; the launch traced here: 23.4 us
  Pallas kernels  22.7 us (97%)
  local copies, waits for them, and re-layouts  0.63 us (3%)
    pallas_call x1, Pallas kernels, local(): pl.pallas_call(kernel, out_shape=pltpu.VMEM((width, quantiles), jnp.float...  22.7 us
    unnamed x1, local copies, waits for them, and re-layouts  0.63 us

profile of v6, /device:TPU:1, one launch (start us, length us, event | category | flops | bytes accessed | tf_op | source)
XLA Modules:
  0.0 23.4 jit_solution(53933658785991197)
XLA Ops:
  0.0 22.7 %shard_map.37 = f32[128,128]{1,0:T(8,128)S(1)} custom-call(s32[1024,128]{1,0:T(8,128)} %bins_hbm.1, f32[32,128]{1,0:T(8,128)} %bitcast.2, f32[1,128]{1,0:T(1,128)} %bitcast.3), custom_call_target="tpu_custom_call" | custom-call | tf_op jit(solution)/shard_map/pallas_call | solution.py:375
  22.7 0.6 %copy.5 = f32[128,128]{1,0:T(8,128)} copy(f32[128,128]{1,0:T(8,128)S(1)} %shard_map.37) | data formatting | bytes 131072
